TPU v7x, 32 devices: a whole 2x2x4 slice. The times are simulated.
32 devices in a mesh: band: 8 (over y, x, core), chan: 4 (over z).
Axes of the slice: x: 2, y: 2, z: 4, core: 2. Of those that a mesh axis runs over, the one named last changes fastest.
Arguments:
- grid_feat: bfloat16 [2048, 468], P('band'), may hold values from -6 to 6
- w_embed: bfloat16 [468, 384], replicated, may hold values from -0.25 to 0.25
- w_send: bfloat16 [384, 384], P(None, 'chan'), may hold values from -0.3125 to 0.3125
- w_recv: bfloat16 [384, 384], P(None, 'chan'), may hold values from -0.3125 to 0.3125
- mesh_nodes: bfloat16 [2048, 384], P('band'), may hold values from -6 to 6
- mesh_cot: bfloat16 [2048, 384], P('band', 'chan'), may hold values from -0.049804688 to 0.049804688
- send_index: int32 [8, 2, 64], P('band'), may hold values from -1 to 255, as said below
- edge_source: int32 [32768], P('band'), may hold values from 0 to 383, as said below
- edge_receiver: int32 [32768], P('band'), may hold values from 0 to 255
Outputs:
- mesh_out: bfloat16 [2048, 384], P('band', 'chan')
- grad_embed: float32 [468, 384], P(None, 'chan')
- grad_send: float32 [384, 384], P(None, 'chan')
- grad_recv: float32 [384, 384], P(None, 'chan')
Inputs may be any that keep to these rules, and one draw needn't show every extreme that they name: `send_index`: A block's first c slots hold rows (c from 32 to 64) and the rest hold -1; block [0, 0] and block [8 - 1, 1] hold only -1; for every band s one of its two blocks that are not all -1 has all 64 slots used (block [0, 1] for band 0, block [8 - 1, 0] for band 8 - 1). `edge_source`: every edge names a used slot of its partition, and every used slot is named by some edge of its partition.
All inputs are finite; a program needn't handle non-finite values.
Results may differ from a plain program's by a relative error of at most 0.011.
Values may be sent and summed in bfloat16 or wider, within the bound.
A program may use at most 64 MiB of HBM per device.

v0:
```python
import functools
import math

import jax
import jax.numpy as jnp
from jax import lax
from jax.experimental import pallas as pl
from jax.experimental.pallas import tpu as pltpu
from jax.sharding import PartitionSpec as P

BF = jnp.bfloat16
F32 = jnp.float32
MESH = pl.DeviceIdType.MESH


def mm(a, b):
    return lax.dot_general(a, b, (((1,), (0,)), ((), ())), preferred_element_type=F32)


def mm_tn(a, b):
    return lax.dot_general(a, b, (((0,), (0,)), ((), ())), preferred_element_type=F32)


def mm_nt(a, b):
    return lax.dot_general(a, b, (((1,), (1,)), ((), ())), preferred_element_type=F32)


def eye(size):
    row = lax.broadcasted_iota(jnp.int32, (size, size), 0)
    col = lax.broadcasted_iota(jnp.int32, (size, size), 1)
    return jnp.where(row == col, 1.0, 0.0).astype(BF)


def sigmoid(v):
    return 0.5 + 0.5 * jnp.tanh(0.5 * v)


def flip(index, bit):
    step = 1 << bit
    return index + step - 2 * step * lax.rem(lax.div(index, step), 2)


def body(
    bands, chans, chunk,
    feat_in, embed_in, wsend_in, wrecv_in, nodes_in, cot_in, send_in, source_in, receiver_in,
    mesh_out, late_out, send_out, recv_out,
    feat, embed, wsend, wrecv, nodes, cot, send, source, receiver, loads,
    latent, back_weight, outgoing, outer, tables, acc, hot_recv, drawn_recv, slots_out, returned, back_out, back_in,
    xs1, xr1, snd1, rcv1, fin1, xs2, xr2, snd2, rcv2, fin2,
    row_send, row_recv, ret_send, ret_recv, back_send, back_recv, sum_send, sum_recv,
):
    band = lax.axis_index("band")
    chan = lax.axis_index("chan")
    bits = bands.bit_length() - 1
    width = wsend.shape[0]
    grid = feat.shape[1]
    mesh_count = nodes.shape[0]
    cap = outgoing.shape[0] // 2
    slots = grid + 2 * cap
    half = width // 2
    left = lax.rem(band + bands - 1, bands)
    right = lax.rem(band + 1, bands)
    partners = [flip(band, bit) for bit in range(bits)]
    others = [lax.rem(chan + step, chans) for step in range(1, chans)]

    barrier = pltpu.get_barrier_semaphore()
    for peer in [left, right] + partners[1:]:
        pl.semaphore_signal(barrier, inc=1, device_id=(peer, chan), device_id_type=MESH)
    for peer in others:
        pl.semaphore_signal(barrier, inc=1, device_id=(band, peer), device_id_type=MESH)

    pulls = {}
    for at, (name, src, dst) in enumerate(
        (
            ("feat", feat_in, feat), ("embed", embed_in, embed), ("send", send_in, send),
            ("wsend", wsend_in, wsend), ("nodes", nodes_in, nodes), ("wrecv", wrecv_in, wrecv),
            ("cot", cot_in, cot), ("source", source_in, source), ("receiver", receiver_in, receiver),
        )
    ):
        pulls[name] = pltpu.make_async_copy(src, dst, loads.at[at])
        pulls[name].start()

    def remote(src, dst, send_sem, recv_sem, to_band, to_chan):
        return pltpu.make_async_remote_copy(
            src_ref=src, dst_ref=dst, send_sem=send_sem, recv_sem=recv_sem,
            device_id=(to_band, to_chan), device_id_type=MESH,
        )

    pulls["send"].wait()
    picks = lax.broadcasted_iota(jnp.int32, (grid, 2 * cap), 0) == jnp.concatenate(
        [send[0, 0:1, :], send[0, 1:2, :]], axis=1
    )
    pick_rows = jnp.transpose(jnp.where(picks, 1.0, 0.0)).astype(BF)
    pulls["feat"].wait()
    pulls["embed"].wait()
    grid_pre = mm_tn(feat[...], embed[...])
    latent[...] = (grid_pre * sigmoid(grid_pre)).astype(BF)
    pulls["wsend"].wait()
    own = mm_nt(wsend[...], latent[...]).astype(BF)
    outgoing[...] = mm_nt(pick_rows, own).astype(BF)
    pl.semaphore_wait(barrier, 2 + (bits - 1) + (chans - 1))
    low, high = pl.ds(0, cap), pl.ds(cap, cap)
    rows = [
        remote(outgoing.at[low], outer.at[high], row_send.at[0], row_recv.at[0], left, chan),
        remote(outgoing.at[high], outer.at[low], row_send.at[1], row_recv.at[1], right, chan),
    ]
    for copy in rows:
        copy.start()

    turn = eye(width)
    for name in ("nodes", "wrecv", "cot", "source", "receiver"):
        pulls[name].wait()
    tables[:width, :grid] = own
    tables[:width, slots:] = mm_nt(wrecv[...], nodes[...]).astype(BF)
    tables[width:, slots:] = cot[...]
    acc[...] = jnp.zeros_like(acc)
    back_weight[...] = mm_nt(eye(wsend.shape[1]), wsend[...]).astype(BF)
    choose = lax.broadcasted_iota(jnp.int32, (width, embed.shape[1]), 1) == (
        lax.broadcasted_iota(jnp.int32, (width, embed.shape[1]), 0) + chan * width
    )
    mine = mm_nt(jnp.where(choose, 1.0, 0.0).astype(BF), embed[...]).astype(BF)
    pre_mine = mm(mine, feat[...])
    gate = sigmoid(pre_mine)
    slope_mine = gate * (1.0 + pre_mine * (1.0 - gate))

    def one_hot(index, count, step):
        at = index[pl.ds(pl.multiple_of(step * chunk, chunk), chunk)].reshape(1, chunk)
        hit = lax.broadcasted_iota(jnp.int32, (count, chunk), 0) == at
        return jnp.where(hit, 1.0, 0.0).astype(BF)

    def receivers(step, carry):
        hot = one_hot(receiver, mesh_count, step)
        hot_recv[step] = hot
        drawn_recv[step] = mm(tables[:, slots:], hot)
        return carry

    steps = source.shape[0] // chunk
    lax.fori_loop(0, steps, receivers, 0)
    for copy in rows:
        copy.wait()
    tables[:width, grid:slots] = mm_nt(turn, outer[...]).astype(BF)

    def edges(step, carry):
        hot = one_hot(source, slots, step)
        pre = mm(tables[:width, :slots], hot) + drawn_recv[step, :width, :]
        gate = sigmoid(pre)
        message = pre * gate
        grad = drawn_recv[step, width:, :] * (gate + message * (1.0 - gate))
        both = jnp.concatenate([message, grad], axis=0).astype(BF)
        acc[width:, :slots] += mm_nt(both[width:], hot)
        acc[:, slots:] += mm_nt(both, hot_recv[step])
        return carry

    lax.fori_loop(0, steps, edges, 0)

    slots_out[...] = mm_nt(eye(2 * cap), acc[width:, grid:slots].astype(BF)).astype(BF)
    backs = [
        remote(slots_out.at[low], returned.at[high], ret_send.at[0], ret_recv.at[0], left, chan),
        remote(slots_out.at[high], returned.at[low], ret_send.at[1], ret_recv.at[1], right, chan),
    ]
    for copy in backs:
        copy.start()
    latents = embed.shape[1]
    xs1[:, :latents] = mm(acc[width:, slots:].astype(BF), nodes[...]).astype(BF)
    mesh_out[...] = acc[:width, slots:].astype(BF)
    for copy in backs:
        copy.wait()
    ret_t = mm_nt(turn, returned[...]).astype(BF)
    total = (acc[width:, :grid].astype(BF).astype(F32) + mm(ret_t, pick_rows)).astype(BF)

    sums = []
    for at, peer in enumerate(others):
        block = back_weight[pl.ds(pl.multiple_of(peer * width, width), width), :]
        back_out[at] = mm(block, total).astype(BF)
        copy = remote(back_out.at[at], back_in.at[at], back_send.at[at], back_recv.at[at], band, peer)
        copy.start()
        sums.append(copy)
    grid_grad = mm(back_weight[pl.ds(pl.multiple_of(chan * width, width), width), :], total)
    xs1[:, latents:] = mm(total, latent[...]).astype(BF)

    my_half = pl.ds(pl.multiple_of(lax.rem(band, 2) * half, half), half)
    its_half = pl.ds(pl.multiple_of((1 - lax.rem(band, 2)) * half, half), half)

    def reduction(base, xs, xr, snd, rcv, fin):
        middle = xs.shape[1] // 2
        copy = remote(
            xs.at[its_half], xr, sum_send.at[base], sum_recv.at[base], partners[0], chan
        )
        copy.start()
        yield
        copy.wait()
        value = xs[my_half, :].astype(F32) + xr[...].astype(F32)
        for at in range(bits - 1):
            snd[at] = value.astype(BF)
            pair = []
            for side, bit in enumerate((1 + at, bits - 1 - at)):
                cut = pl.ds(side * middle, middle)
                sem = base + 1 + 2 * at + side
                pair.append(
                    remote(
                        snd.at[at, :, cut], rcv.at[at, :, cut],
                        sum_send.at[sem], sum_recv.at[sem], partners[bit], chan,
                    )
                )
            for copy in pair:
                copy.start()
            yield
            for copy in pair:
                copy.wait()
            value = snd[at].astype(F32) + rcv[at].astype(F32)
        fin[my_half, :] = value
        sem = base + 1 + 2 * (bits - 1)
        copy = remote(
            fin.at[my_half], fin.at[my_half], sum_send.at[sem], sum_recv.at[sem], partners[0], chan
        )
        copy.start()
        yield
        copy.wait()
        yield

    early = reduction(0, xs1, xr1, snd1, rcv1, fin1)
    late = reduction(2 * bits, xs2, xr2, snd2, rcv2, fin2)
    for _ in range(bits):
        next(early)
    for at, copy in enumerate(sums):
        copy.wait()
        grid_grad = grid_grad + back_in[at].astype(F32)
    pre_grad = (grid_grad * slope_mine).astype(BF)
    inputs = feat.shape[0]
    if inputs < xs2.shape[1]:
        xs2[...] = jnp.zeros_like(xs2)
    xs2[:, :inputs] = mm_nt(pre_grad, feat[...]).astype(BF)
    next(late)
    next(early)
    next(late)
    next(early)
    recv_out[...] = fin1[:, :latents]
    send_out[...] = fin1[:, latents:]
    for _ in range(bits):
        next(late)
    late_out[...] = fin2[:, :inputs]


def place(count, *refs):
    sems = refs[2 * count]
    copies = [
        pltpu.make_async_copy(refs[at], refs[count + at], sems.at[at]) for at in range(count)
    ]
    for copy in copies:
        copy.start()
    for copy in copies:
        copy.wait()


def on_device(
    grid_feat, w_embed, w_send, w_recv, mesh_nodes, mesh_cot, send_index, edge_source, edge_receiver
):
    bands = lax.axis_size("band")
    chans = lax.axis_size("chan")
    bits = bands.bit_length() - 1
    grid, inputs = grid_feat.shape
    latents, width = w_send.shape
    mesh_count = mesh_nodes.shape[0]
    cap = send_index.shape[2]
    slots = grid + 2 * cap
    half = width // 2
    chunk = math.gcd(edge_source.shape[0], 1024)
    wide1 = 2 * latents
    wide2 = -(-inputs // 256) * 256
    steps = max(bits - 1, 1)
    vmem = pl.BlockSpec(memory_space=pltpu.VMEM)
    arrays = (
        grid_feat.T, w_embed, w_send.T, w_recv.T, mesh_nodes, mesh_cot.T,
        send_index, edge_source, edge_receiver,
    )
    outs = pl.pallas_call(
        functools.partial(body, bands, chans, chunk),
        out_shape=(
            pltpu.VMEM((width, mesh_count), BF),
            pltpu.VMEM((width, inputs), F32),
            pltpu.VMEM((width, latents), F32),
            pltpu.VMEM((width, latents), F32),
        ),
        in_specs=[pl.BlockSpec(memory_space=pl.ANY)] * 9,
        out_specs=(vmem,) * 4,
        scratch_shapes=[
            pltpu.VMEM(array.shape, array.dtype) for array in arrays
        ]
        + [
            pltpu.SemaphoreType.DMA((9,)),
            pltpu.VMEM((grid, latents), BF),
            pltpu.VMEM((latents, width), BF),
            pltpu.VMEM((2 * cap, width), BF),
            pltpu.VMEM((2 * cap, width), BF),
            pltpu.VMEM((2 * width, slots + mesh_count), BF),
            pltpu.VMEM((2 * width, slots + mesh_count), F32),
            pltpu.VMEM((edge_source.shape[0] // chunk, mesh_count, chunk), BF),
            pltpu.VMEM((edge_source.shape[0] // chunk, 2 * width, chunk), F32),
            pltpu.VMEM((2 * cap, width), BF),
            pltpu.VMEM((2 * cap, width), BF),
            pltpu.VMEM((chans - 1, width, grid), BF),
            pltpu.VMEM((chans - 1, width, grid), BF),
        ]
        + [
            pltpu.VMEM(shape, kind)
            for wide in (wide1, wide2)
            for shape, kind in (
                ((width, wide), BF),
                ((half, wide), BF),
                ((steps, half, wide), BF),
                ((steps, half, wide), BF),
                ((width, wide), F32),
            )
        ]
        + [
            pltpu.SemaphoreType.DMA((count,))
            for count in (2, 2, 2, 2, chans - 1, chans - 1, 4 * bits, 4 * bits)
        ],
        compiler_params=pltpu.CompilerParams(collective_id=0, has_side_effects=True),
    )(*arrays)
    anywhere = pl.BlockSpec(memory_space=pl.ANY)
    placed = pl.pallas_call(
        functools.partial(place, len(outs)),
        out_shape=tuple(jax.ShapeDtypeStruct(out.shape, out.dtype) for out in outs),
        in_specs=[vmem] * len(outs),
        out_specs=(anywhere,) * len(outs),
        scratch_shapes=[pltpu.SemaphoreType.DMA((len(outs),))],
    )(*(pltpu.with_memory_space_constraint(out, pltpu.VMEM) for out in outs))
    return tuple(out.T for out in placed)


def solution(mesh):
    placed = (
        P("band", None),
        P(),
        P(None, "chan"),
        P(None, "chan"),
        P("band", None),
        P("band", "chan"),
        P("band", None, None),
        P("band"),
        P("band"),
    )
    return jax.shard_map(
        on_device,
        mesh=mesh,
        in_specs=placed,
        out_specs=(P("band", "chan"), P(None, "chan"), P(None, "chan"), P(None, "chan")),
        check_vma=False,
    )
```

profile of v0, /device:TPU:0, one launch (start us, length us, event | category | flops | bytes accessed | tf_op | source)
XLA Modules:
  0.0 31.0 jit_solution(7776617991377936539)
XLA Ops:
  0.6 29.6 %shard_map.120 = (bf16[96,256]{1,0:T(8,128)(2,1)S(1)}, f32[96,468]{1,0:T(8,128)S(1)}, f32[96,384]{1,0:T(8,128)S(1)}, f32[96,384]{1,0:T(8,128)S(1)}) custom-call(bf16[468,256]{1,0:T(8,128)(2,1)} %bitcast.8, bf16[468,384]{1,0:T(8,128)(2,1)} %embed_in.1, bf16[96,384]{1,0:T(8,128)(2,1)} %bitcast.9, bf16[96,384]{1,0:T(8,128)(2,1)} %bitcast.10, ...), custom_call_target="tpu_custom_call" | custom-call | tf_op jit(solution)/shard_map/pallas_call | solution.py:276
  30.2 0.8 %shard_map.121 = (bf16[96,256]{1,0:T(8,128)(2,1)}, f32[96,468]{1,0:T(8,128)}, f32[96,384]{1,0:T(8,128)}, f32[96,384]{1,0:T(8,128)}) custom-call(bf16[96,256]{1,0:T(8,128)(2,1)S(1)} %get-tuple-element.12.refs_0_, f32[96,468]{1,0:T(8,128)S(1)} %get-tuple-element.13.refs_1_, f32[96,384]{1,0:T(8,128)S(1)} %get-tuple-element.14.refs_2_, ...), custom_call_target="tpu_custom_call" | custom-call | tf_op jit(solution)/shard_map/pallas_call | solution.py:322
where the time goes:
time: 31.2 us; the launch traced here: 31 us
  Pallas kernels  30.4 us (97%)
  between operations  0.64 us (2%)
    pallas_call x1, Pallas kernels, on_device(): pl.pallas_call(functools.partial(body, bands, chans, chunk), out_shape=(p...  29.6 us
    pallas_call x1, Pallas kernels, on_device(): pl.pallas_call(functools.partial(place, len(outs)), out_shape=tuple((jax....  0.83 us

commit v1 on v0

v1 whole, which is shorter than its diff:
```python
import functools
import math

import jax
import jax.numpy as jnp
from jax import lax
from jax.experimental import pallas as pl
from jax.experimental.pallas import tpu as pltpu
from jax.sharding import PartitionSpec as P

BF = jnp.bfloat16
F32 = jnp.float32
MESH = pl.DeviceIdType.MESH
LANES = 128


def mm(a, b):
    return lax.dot_general(a, b, (((1,), (0,)), ((), ())), preferred_element_type=F32)


def mm_tn(a, b):
    return lax.dot_general(a, b, (((0,), (0,)), ((), ())), preferred_element_type=F32)


def mm_nt(a, b):
    return lax.dot_general(a, b, (((1,), (1,)), ((), ())), preferred_element_type=F32)


def eye(size):
    row = lax.broadcasted_iota(jnp.int32, (size, size), 0)
    col = lax.broadcasted_iota(jnp.int32, (size, size), 1)
    return jnp.where(row == col, 1.0, 0.0).astype(BF)


def sigmoid(v):
    return 0.5 + 0.5 * jnp.tanh(0.5 * v)


def body(
    bands, chans, chunk,
    feat_in, embed_in, wsend_in, wrecv_in, nodes_in, cot_in, send_in, source_in, receiver_in,
    mesh_out, late_out, send_out, recv_out,
    feat, embed, wsend, wrecv, nodes, cot, send, source, receiver, loads,
    latent, slope, outgoing, outer, feat_out, feat_rows, latent_rows, slope_rows,
    tables, hot_recv, hot_src, drawn, pairs, acc, total,
    part_own, part_out, part_in, z_out, z_in, planes, final,
    e_own, e_out, e_in, e_planes, e_final,
    row_send, row_recv, feat_send, feat_recv, part_send, part_recv, z_send, z_recv,
    plane_send, plane_recv, final_send, final_recv, e_send, e_recv, ep_send, ep_recv, ef_send, ef_recv,
):
    band = lax.axis_index("band")
    chan = lax.axis_index("chan")
    chips = bands // 2
    core = lax.rem(band, 2)
    chip = lax.div(band, 2)
    width = wsend.shape[0]
    grid = feat.shape[1]
    inputs = feat.shape[0]
    latents = embed.shape[1]
    mesh_count = nodes.shape[0]
    cap = outgoing.shape[0] // 2
    slots = grid + 2 * cap
    steps = source.shape[0] // chunk
    cuts = [(at, min(at + LANES, inputs)) for at in range(0, inputs, LANES)]
    left = lax.rem(band + bands - 1, bands)
    right = lax.rem(band + 1, bands)
    mate = band + 1 - 2 * core
    peers = [2 * lax.rem(chip + step, chips) + core for step in range(1, chips)]
    others = [lax.rem(chan + step, chans) for step in range(1, chans)]

    barrier = pltpu.get_barrier_semaphore()
    for peer in [left, right, mate] + peers:
        pl.semaphore_signal(barrier, inc=1, device_id=(peer, chan), device_id_type=MESH)
    for peer in others:
        pl.semaphore_signal(barrier, inc=1, device_id=(band, peer), device_id_type=MESH)

    pulls = {}
    for at, (name, src, dst) in enumerate(
        (
            ("send", send_in, send), ("feat", feat_in, feat), ("embed", embed_in, embed),
            ("wsend", wsend_in, wsend), ("nodes", nodes_in, nodes), ("wrecv", wrecv_in, wrecv),
            ("cot", cot_in, cot), ("source", source_in, source), ("receiver", receiver_in, receiver),
        )
    ):
        pulls[name] = pltpu.make_async_copy(src, dst, loads.at[at])
        pulls[name].start()

    def remote(src, dst, send_sem, recv_sem, to_band, to_chan):
        return pltpu.make_async_remote_copy(
            src_ref=src, dst_ref=dst, send_sem=send_sem, recv_sem=recv_sem,
            device_id=(to_band, to_chan), device_id_type=MESH,
        )

    pulls["send"].wait()
    picks = lax.broadcasted_iota(jnp.int32, (grid, 2 * cap), 0) == jnp.concatenate(
        [send[0, 0:1, :], send[0, 1:2, :]], axis=1
    )
    pick_rows = jnp.transpose(jnp.where(picks, 1.0, 0.0)).astype(BF)
    pulls["feat"].wait()
    pulls["embed"].wait()
    pre = mm_tn(embed[...], feat[...])
    gate = sigmoid(pre)
    silu = pre * gate
    latent[...] = silu.astype(BF)
    slope[...] = gate + silu * (1.0 - gate)
    pulls["wsend"].wait()
    own = mm(wsend[...], latent[...]).astype(BF)
    outgoing[...] = mm_nt(pick_rows, own).astype(BF)
    if inputs < feat_out.shape[1]:
        feat_out[...] = jnp.zeros_like(feat_out)
    feat_out[:, :inputs] = mm_nt(pick_rows, feat[...]).astype(BF)
    pl.semaphore_wait(barrier, 3 + (chips - 1) + (chans - 1))
    low, high = pl.ds(0, cap), pl.ds(cap, cap)
    rows = [
        remote(outgoing.at[low], outer.at[high], row_send.at[0], row_recv.at[0], left, chan),
        remote(outgoing.at[high], outer.at[low], row_send.at[1], row_recv.at[1], right, chan),
    ]
    feats = [
        remote(feat_out.at[low], feat_rows.at[high], feat_send.at[0], feat_recv.at[0], left, chan),
        remote(feat_out.at[high], feat_rows.at[low], feat_send.at[1], feat_recv.at[1], right, chan),
    ]
    for copy in rows + feats:
        copy.start()

    turn = eye(width)
    for name in ("nodes", "wrecv", "cot", "source", "receiver"):
        pulls[name].wait()
    tables[:width, :grid] = own
    tables[:width, slots:] = mm_nt(wrecv[...], nodes[...]).astype(BF)
    tables[width:, slots:] = cot[...]

    def one_hot(index, count, step):
        at = index[pl.ds(step * chunk, chunk)].reshape(1, chunk)
        hit = lax.broadcasted_iota(jnp.int32, (count, chunk), 0) == at
        return jnp.where(hit, 1.0, 0.0).astype(BF)

    for step in range(steps):
        hot_recv[step] = one_hot(receiver, mesh_count, step)
        drawn[step] = mm(tables[:, slots:], hot_recv[step])
        hot_src[step] = one_hot(source, slots, step)
        drawn[step, :width, :] += mm(tables[:width, :grid], hot_src[step, :grid, :])
    for copy in rows:
        copy.wait_recv()
    tables[:width, grid:slots] = mm_nt(turn, outer[...]).astype(BF)

    for step in range(steps):
        pre = drawn[step, :width, :] + mm(tables[:width, grid:slots], hot_src[step, grid:, :])
        gate = sigmoid(pre)
        message = pre * gate
        grad = (drawn[step, width:, :] * (gate + message * (1.0 - gate))).astype(BF)
        pairs[step, :width, :] = message.astype(BF)
        pairs[step, width:, :] = grad
        mine = mm_nt(grad, hot_src[step])
        if step == 0:
            acc[...] = mine
        else:
            acc[...] += mine
    total[...] = acc[...].astype(BF)

    for copy in feats:
        copy.wait_recv()
    pre = mm(feat_rows[:, :inputs], embed[...])
    gate = sigmoid(pre)
    silu = pre * gate
    latent_rows[...] = silu.astype(BF)
    slope_rows[...] = gate + silu * (1.0 - gate)
    back = (mm_tn(wsend[...], total[:, :grid]) * slope[...]).astype(BF)
    back_rows = (mm_tn(total[:, grid:], wsend[...]) * slope_rows[...]).astype(BF)

    def partial(lo, hi):
        return mm_nt(back, feat[lo:hi, :]) + mm_tn(back_rows, feat_rows[:, lo:hi])

    def receiver_sums():
        sums = mm_nt(pairs[0], hot_recv[0])
        for step in range(1, steps):
            sums += mm_nt(pairs[step], hot_recv[step])
        mesh_out[...] = sums[:width].astype(BF)
        e_own[:, :latents] = mm(sums[width:].astype(BF), nodes[...])
        e_own[:, latents:] = mm_nt(total[:, :grid], latent[...]) + mm(total[:, grid:], latent_rows[...])

    part_copies = [
        remote(part_out.at[at], part_in.at[at], part_send.at[at], part_recv.at[at], mate, chan)
        for at in range(len(cuts))
    ]
    e_copy = remote(e_out, e_in, e_send.at[0], e_recv.at[0], mate, chan)
    final_copies = [
        remote(final.at[at], final.at[at], final_send.at[at], final_recv.at[at], mate, chan)
        for at in range(len(cuts))
    ]
    ef_copy = remote(e_final, e_final, ef_send.at[0], ef_recv.at[0], mate, chan)

    @pl.when(core == 0)
    def _():
        for at, (lo, hi) in enumerate(cuts):
            if hi - lo < LANES:
                part_out[at] = jnp.zeros_like(part_out[at])
            part_out[at, :, : hi - lo] = partial(lo, hi).astype(BF)
            part_copies[at].start()
        receiver_sums()
        e_copy.wait_recv()
        e_planes[chip] = (e_own[...] + e_in[...].astype(F32)).astype(BF)
        copies = [
            remote(e_planes.at[chip], e_planes.at[chip], ep_send.at[at], ep_recv.at[at], peer, chan)
            for at, peer in enumerate(peers)
        ]
        for copy in copies:
            copy.start()
        for copy in copies:
            copy.wait_recv()
        value = e_planes[0].astype(F32)
        for at in range(1, chips):
            value += e_planes[at].astype(F32)
        e_final[...] = value
        ef_copy.start()
        for at, (lo, hi) in enumerate(cuts):
            final_copies[at].wait_recv()
            late_out[:, lo:hi] = final[at, :, : hi - lo]
        for copy in part_copies + copies + [ef_copy]:
            copy.wait_send()

    @pl.when(core == 1)
    def _():
        mine = pl.ds(pl.multiple_of(chan * width, width), width)
        for at, (lo, hi) in enumerate(cuts):
            part_own[at, :, : hi - lo] = partial(lo, hi)
        receiver_sums()
        e_out[...] = e_own[...].astype(BF)
        e_copy.start()
        moves = []
        for at, (lo, hi) in enumerate(cuts):
            part_copies[at].wait_recv()
            if hi - lo < LANES:
                z_out[at] = jnp.zeros_like(z_out[at])
            wide = slice(0, hi - lo)
            z_out[at, :, wide] = (part_own[at, :, wide] + part_in[at, :, wide].astype(F32)).astype(BF)
            moves.append([])
            for step, peer in enumerate(others):
                block = pl.ds(pl.multiple_of(peer * width, width), width)
                copy = remote(
                    z_out.at[at, block], z_in.at[at, step], z_send.at[at, step], z_recv.at[at, step], band, peer
                )
                copy.start()
                moves[at].append(copy)
        swaps = []
        for at, (lo, hi) in enumerate(cuts):
            value = z_out[at, mine, :].astype(F32)
            for step, copy in enumerate(moves[at]):
                copy.wait_recv()
                value += z_in[at, step].astype(F32)
            planes[at, chip] = value.astype(BF)
            swaps.append([])
            for step, peer in enumerate(peers):
                copy = remote(
                    planes.at[at, chip], planes.at[at, chip], plane_send.at[at, step], plane_recv.at[at, step],
                    peer, chan,
                )
                copy.start()
                swaps[at].append(copy)
        for at, (lo, hi) in enumerate(cuts):
            for copy in swaps[at]:
                copy.wait_recv()
            value = planes[at, 0].astype(F32)
            for other in range(1, chips):
                value += planes[at, other].astype(F32)
            final[at] = value
            final_copies[at].start()
            late_out[:, lo:hi] = value[:, : hi - lo]
        ef_copy.wait_recv()
        for copy in [e_copy] + final_copies + sum(moves, []) + sum(swaps, []):
            copy.wait_send()

    recv_out[...] = e_final[:, :latents]
    send_out[...] = e_final[:, latents:]
    for copy in rows + feats:
        copy.wait_send()


def place(count, *refs):
    sems = refs[2 * count]
    copies = [
        pltpu.make_async_copy(refs[at], refs[count + at], sems.at[at]) for at in range(count)
    ]
    for copy in copies:
        copy.start()
    for copy in copies:
        copy.wait()


def on_device(
    grid_feat, w_embed, w_send, w_recv, mesh_nodes, mesh_cot, send_index, edge_source, edge_receiver
):
    bands = lax.axis_size("band")
    chans = lax.axis_size("chan")
    chips = bands // 2
    grid, inputs = grid_feat.shape
    latents, width = w_send.shape
    mesh_count = mesh_nodes.shape[0]
    cap = send_index.shape[2]
    slots = grid + 2 * cap
    edges = edge_source.shape[0]
    chunk = math.gcd(edges, 1024)
    steps = edges // chunk
    cuts = -(-inputs // LANES)
    wide = cuts * LANES
    vmem = pl.BlockSpec(memory_space=pltpu.VMEM)
    arrays = (
        grid_feat.T, w_embed, w_send.T, w_recv.T, mesh_nodes, mesh_cot.T,
        send_index, edge_source, edge_receiver,
    )
    scratch = [
        ((latents, grid), BF),
        ((latents, grid), F32),
        ((2 * cap, width), BF),
        ((2 * cap, width), BF),
        ((2 * cap, wide), BF),
        ((2 * cap, wide), BF),
        ((2 * cap, latents), BF),
        ((2 * cap, latents), F32),
        ((2 * width, slots + mesh_count), BF),
        ((steps, mesh_count, chunk), BF),
        ((steps, slots, chunk), BF),
        ((steps, 2 * width, chunk), F32),
        ((steps, 2 * width, chunk), BF),
        ((width, slots), F32),
        ((width, slots), BF),
        ((cuts, latents, LANES), F32),
        ((cuts, latents, LANES), BF),
        ((cuts, latents, LANES), BF),
        ((cuts, latents, LANES), BF),
        ((cuts, chans - 1, width, LANES), BF),
        ((cuts, chips, width, LANES), BF),
        ((cuts, width, LANES), F32),
        ((width, 2 * latents), F32),
        ((width, 2 * latents), BF),
        ((width, 2 * latents), BF),
        ((chips, width, 2 * latents), BF),
        ((width, 2 * latents), F32),
    ]
    sems = [
        (2,), (2,), (2,), (2,), (cuts,), (cuts,), (cuts, chans - 1), (cuts, chans - 1),
        (cuts, chips - 1), (cuts, chips - 1), (cuts,), (cuts,), (1,), (1,), (chips - 1,), (chips - 1,), (1,), (1,),
    ]
    outs = pl.pallas_call(
        functools.partial(body, bands, chans, chunk),
        out_shape=(
            pltpu.VMEM((width, mesh_count), BF),
            pltpu.VMEM((width, inputs), F32),
            pltpu.VMEM((width, latents), F32),
            pltpu.VMEM((width, latents), F32),
        ),
        in_specs=[pl.BlockSpec(memory_space=pl.ANY)] * 9,
        out_specs=(vmem,) * 4,
        scratch_shapes=[pltpu.VMEM(array.shape, array.dtype) for array in arrays]
        + [pltpu.SemaphoreType.DMA((9,))]
        + [pltpu.VMEM(shape, kind) for shape, kind in scratch]
        + [pltpu.SemaphoreType.DMA(shape) for shape in sems],
        compiler_params=pltpu.CompilerParams(collective_id=0, has_side_effects=True),
    )(*arrays)
    anywhere = pl.BlockSpec(memory_space=pl.ANY)
    placed = pl.pallas_call(
        functools.partial(place, len(outs)),
        out_shape=tuple(jax.ShapeDtypeStruct(out.shape, out.dtype) for out in outs),
        in_specs=[vmem] * len(outs),
        out_specs=(anywhere,) * len(outs),
        scratch_shapes=[pltpu.SemaphoreType.DMA((len(outs),))],
    )(*(pltpu.with_memory_space_constraint(out, pltpu.VMEM) for out in outs))
    return tuple(out.T for out in placed)


def solution(mesh):
    placed = (
        P("band", None),
        P(),
        P(None, "chan"),
        P(None, "chan"),
        P("band", None),
        P("band", "chan"),
        P("band", None, None),
        P("band"),
        P("band"),
    )
    return jax.shard_map(
        on_device,
        mesh=mesh,
        in_specs=placed,
        out_specs=(P("band", "chan"), P(None, "chan"), P(None, "chan"), P(None, "chan")),
        check_vma=False,
    )
```

time: 31.2 us -> 24.7 us (0.79)
  Pallas kernels: 30.4 us -> 23.9 us
    pallas_call x1, Pallas kernels: 29.6 us -> 23.1 us  [on_device(): pl.pallas_call(functools.partial(body, bands, chans, chunk), out_shape=(p...]
where the time goes in v1:
time: 24.7 us; the launch traced here: 24.6 us
  Pallas kernels  23.9 us (97%)
  between operations  0.64 us (3%)
    pallas_call x1, Pallas kernels, on_device(): pl.pallas_call(functools.partial(body, bands, chans, chunk), out_shape=(p...  23.1 us
    pallas_call x1, Pallas kernels, on_device(): pl.pallas_call(functools.partial(place, len(outs)), out_shape=tuple((jax....  0.83 us

profile of v1, /device:TPU:0, one launch (start us, length us, event | category | flops | bytes accessed | tf_op | source)
XLA Modules:
  0.0 24.6 jit_solution(10743836177072685167)
XLA Ops:
  0.6 23.1 %shard_map.120 = (bf16[96,256]{1,0:T(8,128)(2,1)S(1)}, f32[96,468]{1,0:T(8,128)S(1)}, f32[96,384]{1,0:T(8,128)S(1)}, f32[96,384]{1,0:T(8,128)S(1)}) custom-call(bf16[468,256]{1,0:T(8,128)(2,1)} %bitcast.8, bf16[468,384]{1,0:T(8,128)(2,1)} %embed_in.1, bf16[96,384]{1,0:T(8,128)(2,1)} %bitcast.9, bf16[96,384]{1,0:T(8,128)(2,1)} %bitcast.10, ...), custom_call_target="tpu_custom_call" | custom-call | tf_op jit(solution)/shard_map/pallas_call | solution.py:343
  23.7 0.8 %shard_map.121 = (bf16[96,256]{1,0:T(8,128)(2,1)}, f32[96,468]{1,0:T(8,128)}, f32[96,384]{1,0:T(8,128)}, f32[96,384]{1,0:T(8,128)}) custom-call(bf16[96,256]{1,0:T(8,128)(2,1)S(1)} %get-tuple-element.12.refs_0_, f32[96,468]{1,0:T(8,128)S(1)} %get-tuple-element.13.refs_1_, f32[96,384]{1,0:T(8,128)S(1)} %get-tuple-element.14.refs_2_, ...), custom_call_target="tpu_custom_call" | custom-call | tf_op jit(solution)/shard_map/pallas_call | solution.py:360

commit v2 on v1

--- a/solution.py
+++ b/solution.py
@@ -41,10 +41,10 @@
     feat_in, embed_in, wsend_in, wrecv_in, nodes_in, cot_in, send_in, source_in, receiver_in,
     mesh_out, late_out, send_out, recv_out,
     feat, embed, wsend, wrecv, nodes, cot, send, source, receiver, loads,
-    latent, slope, outgoing, outer, feat_out, feat_rows, latent_rows, slope_rows,
+    embed_t, wsend_t, latent, slope, back, outgoing, outer, feat_out, feat_rows,
     tables, hot_recv, hot_src, drawn, pairs, acc, total,
     part_own, part_out, part_in, z_out, z_in, planes, final,
-    e_own, e_out, e_in, e_planes, e_final,
+    e_out, e_in, e_planes, e_final,
     row_send, row_recv, feat_send, feat_recv, part_send, part_recv, z_send, z_recv,
     plane_send, plane_recv, final_send, final_recv, e_send, e_recv, ep_send, ep_recv, ef_send, ef_recv,
 ):
@@ -67,12 +67,7 @@
     mate = band + 1 - 2 * core
     peers = [2 * lax.rem(chip + step, chips) + core for step in range(1, chips)]
     others = [lax.rem(chan + step, chans) for step in range(1, chans)]
-
-    barrier = pltpu.get_barrier_semaphore()
-    for peer in [left, right, mate] + peers:
-        pl.semaphore_signal(barrier, inc=1, device_id=(peer, chan), device_id_type=MESH)
-    for peer in others:
-        pl.semaphore_signal(barrier, inc=1, device_id=(band, peer), device_id_type=MESH)
+    ordered = [step + lax.min(lax.max(step + 1 - chan, 0), 1) for step in range(chans - 1)]
 
     pulls = {}
     for at, (name, src, dst) in enumerate(
@@ -85,6 +80,12 @@
         pulls[name] = pltpu.make_async_copy(src, dst, loads.at[at])
         pulls[name].start()
 
+    barrier = pltpu.get_barrier_semaphore()
+    for peer in [left, right, mate] + peers:
+        pl.semaphore_signal(barrier, inc=1, device_id=(peer, chan), device_id_type=MESH)
+    for peer in others:
+        pl.semaphore_signal(barrier, inc=1, device_id=(band, peer), device_id_type=MESH)
+
     def remote(src, dst, send_sem, recv_sem, to_band, to_chan):
         return pltpu.make_async_remote_copy(
             src_ref=src, dst_ref=dst, send_sem=send_sem, recv_sem=recv_sem,
@@ -101,27 +102,30 @@
     pre = mm_tn(embed[...], feat[...])
     gate = sigmoid(pre)
     silu = pre * gate
-    latent[...] = silu.astype(BF)
-    slope[...] = gate + silu * (1.0 - gate)
+    latent[:, :grid] = silu.astype(BF)
     pulls["wsend"].wait()
-    own = mm(wsend[...], latent[...]).astype(BF)
+    own = mm(wsend[...], latent[:, :grid]).astype(BF)
     outgoing[...] = mm_nt(pick_rows, own).astype(BF)
-    if inputs < feat_out.shape[1]:
-        feat_out[...] = jnp.zeros_like(feat_out)
-    feat_out[:, :inputs] = mm_nt(pick_rows, feat[...]).astype(BF)
     pl.semaphore_wait(barrier, 3 + (chips - 1) + (chans - 1))
     low, high = pl.ds(0, cap), pl.ds(cap, cap)
     rows = [
         remote(outgoing.at[low], outer.at[high], row_send.at[0], row_recv.at[0], left, chan),
         remote(outgoing.at[high], outer.at[low], row_send.at[1], row_recv.at[1], right, chan),
     ]
+    for copy in rows:
+        copy.start()
+    if inputs < feat_out.shape[1]:
+        feat_out[...] = jnp.zeros_like(feat_out)
+    feat_out[:, :inputs] = mm_nt(pick_rows, feat[...]).astype(BF)
     feats = [
         remote(feat_out.at[low], feat_rows.at[high], feat_send.at[0], feat_recv.at[0], left, chan),
         remote(feat_out.at[high], feat_rows.at[low], feat_send.at[1], feat_recv.at[1], right, chan),
     ]
-    for copy in rows + feats:
+    for copy in feats:
         copy.start()
 
+    slope[:, :grid] = gate + silu * (1.0 - gate)
+    wsend_t[...] = mm_nt(eye(latents), wsend[...]).astype(BF)
     turn = eye(width)
     for name in ("nodes", "wrecv", "cot", "source", "receiver"):
         pulls[name].wait()
@@ -132,13 +136,14 @@
     def one_hot(index, count, step):
         at = index[pl.ds(step * chunk, chunk)].reshape(1, chunk)
         hit = lax.broadcasted_iota(jnp.int32, (count, chunk), 0) == at
-        return jnp.where(hit, 1.0, 0.0).astype(BF)
+        return jnp.where(hit, 1.0, 0.0).astype(jnp.float8_e4m3fn)
 
     for step in range(steps):
         hot_recv[step] = one_hot(receiver, mesh_count, step)
         drawn[step] = mm(tables[:, slots:], hot_recv[step])
         hot_src[step] = one_hot(source, slots, step)
         drawn[step, :width, :] += mm(tables[:width, :grid], hot_src[step, :grid, :])
+    embed_t[...] = jnp.transpose(embed[...])
     for copy in rows:
         copy.wait_recv()
     tables[:width, grid:slots] = mm_nt(turn, outer[...]).astype(BF)
@@ -159,73 +164,91 @@
 
     for copy in feats:
         copy.wait_recv()
-    pre = mm(feat_rows[:, :inputs], embed[...])
+    pre = mm_nt(embed_t[...], feat_rows[:, :inputs])
     gate = sigmoid(pre)
     silu = pre * gate
-    latent_rows[...] = silu.astype(BF)
-    slope_rows[...] = gate + silu * (1.0 - gate)
-    back = (mm_tn(wsend[...], total[:, :grid]) * slope[...]).astype(BF)
-    back_rows = (mm_tn(total[:, grid:], wsend[...]) * slope_rows[...]).astype(BF)
+    latent[:, grid:] = silu.astype(BF)
+    slope[:, grid:] = gate + silu * (1.0 - gate)
+
+    def gradients():
+        back[...] = (mm(wsend_t[...], total[...]) * slope[...]).astype(BF)
 
     def partial(lo, hi):
-        return mm_nt(back, feat[lo:hi, :]) + mm_tn(back_rows, feat_rows[:, lo:hi])
-
-    def receiver_sums():
+        return mm_nt(back[:, :grid], feat[lo:hi, :]) + mm(back[:, grid:], feat_rows[:, lo:hi])
+
+    def sender_part():
+        return mm_nt(total[...], latent[...])
+
+    def receiver_part():
         sums = mm_nt(pairs[0], hot_recv[0])
         for step in range(1, steps):
             sums += mm_nt(pairs[step], hot_recv[step])
         mesh_out[...] = sums[:width].astype(BF)
-        e_own[:, :latents] = mm(sums[width:].astype(BF), nodes[...])
-        e_own[:, latents:] = mm_nt(total[:, :grid], latent[...]) + mm(total[:, grid:], latent_rows[...])
+        return mm(sums[width:].astype(BF), nodes[...])
 
     part_copies = [
         remote(part_out.at[at], part_in.at[at], part_send.at[at], part_recv.at[at], mate, chan)
         for at in range(len(cuts))
     ]
-    e_copy = remote(e_out, e_in, e_send.at[0], e_recv.at[0], mate, chan)
+    sides = ((sender_part, send_out), (receiver_part, recv_out))
+    e_copies = [
+        remote(e_out.at[at], e_in.at[at], e_send.at[at], e_recv.at[at], mate, chan) for at in range(2)
+    ]
+    ef_copies = [
+        remote(e_final.at[at], e_final.at[at], ef_send.at[at], ef_recv.at[at], mate, chan) for at in range(2)
+    ]
     final_copies = [
         remote(final.at[at], final.at[at], final_send.at[at], final_recv.at[at], mate, chan)
         for at in range(len(cuts))
     ]
-    ef_copy = remote(e_final, e_final, ef_send.at[0], ef_recv.at[0], mate, chan)
 
     @pl.when(core == 0)
     def _():
+        gradients()
         for at, (lo, hi) in enumerate(cuts):
             if hi - lo < LANES:
                 part_out[at] = jnp.zeros_like(part_out[at])
             part_out[at, :, : hi - lo] = partial(lo, hi).astype(BF)
             part_copies[at].start()
-        receiver_sums()
-        e_copy.wait_recv()
-        e_planes[chip] = (e_own[...] + e_in[...].astype(F32)).astype(BF)
-        copies = [
-            remote(e_planes.at[chip], e_planes.at[chip], ep_send.at[at], ep_recv.at[at], peer, chan)
-            for at, peer in enumerate(peers)
-        ]
-        for copy in copies:
-            copy.start()
-        for copy in copies:
-            copy.wait_recv()
-        value = e_planes[0].astype(F32)
-        for at in range(1, chips):
-            value += e_planes[at].astype(F32)
-        e_final[...] = value
-        ef_copy.start()
+        copies = []
+        for side, (own_part, _) in enumerate(sides):
+            value = own_part()
+            e_copies[side].wait_recv()
+            e_planes[side, chip] = (value + e_in[side].astype(F32)).astype(BF)
+            copies.append([])
+            for at, peer in enumerate(peers):
+                copy = remote(
+                    e_planes.at[side, chip], e_planes.at[side, chip], ep_send.at[side, at], ep_recv.at[side, at],
+                    peer, chan,
+                )
+                copy.start()
+                copies[side].append(copy)
+        for side, (_, out) in enumerate(sides):
+            for copy in copies[side]:
+                copy.wait_recv()
+            value = e_planes[side, 0].astype(F32)
+            for at in range(1, chips):
+                value += e_planes[side, at].astype(F32)
+            e_final[side] = value
+            ef_copies[side].start()
+            out[...] = value
         for at, (lo, hi) in enumerate(cuts):
             final_copies[at].wait_recv()
             late_out[:, lo:hi] = final[at, :, : hi - lo]
-        for copy in part_copies + copies + [ef_copy]:
+        for copy in part_copies + sum(copies, []) + ef_copies:
             copy.wait_send()
 
     @pl.when(core == 1)
     def _():
         mine = pl.ds(pl.multiple_of(chan * width, width), width)
+        first = pl.ds(pl.multiple_of(ordered[0] * width, width), width)
+        e_out[0] = sender_part().astype(BF)
+        e_copies[0].start()
+        gradients()
         for at, (lo, hi) in enumerate(cuts):
             part_own[at, :, : hi - lo] = partial(lo, hi)
-        receiver_sums()
-        e_out[...] = e_own[...].astype(BF)
-        e_copy.start()
+        e_out[1] = receiver_part().astype(BF)
+        e_copies[1].start()
         moves = []
         for at, (lo, hi) in enumerate(cuts):
             part_copies[at].wait_recv()
@@ -233,20 +256,27 @@
                 z_out[at] = jnp.zeros_like(z_out[at])
             wide = slice(0, hi - lo)
             z_out[at, :, wide] = (part_own[at, :, wide] + part_in[at, :, wide].astype(F32)).astype(BF)
-            moves.append([])
-            for step, peer in enumerate(others):
-                block = pl.ds(pl.multiple_of(peer * width, width), width)
+            copy = remote(
+                z_out.at[at, first], z_in.at[at, chan], z_send.at[at, 0], z_recv.at[at, chan], band, ordered[0]
+            )
+            copy.start()
+            moves.append(copy)
+        for step, peer in enumerate(ordered[1:], 1):
+            block = pl.ds(pl.multiple_of(peer * width, width), width)
+            for at in range(len(cuts)):
                 copy = remote(
-                    z_out.at[at, block], z_in.at[at, step], z_send.at[at, step], z_recv.at[at, step], band, peer
+                    z_out.at[at, block], z_in.at[at, chan], z_send.at[at, step], z_recv.at[at, chan], band, peer
                 )
                 copy.start()
-                moves[at].append(copy)
+                moves.append(copy)
         swaps = []
         for at, (lo, hi) in enumerate(cuts):
             value = z_out[at, mine, :].astype(F32)
-            for step, copy in enumerate(moves[at]):
-                copy.wait_recv()
-                value += z_in[at, step].astype(F32)
+            for step, peer in enumerate(ordered):
+                remote(
+                    z_out.at[at, mine], z_in.at[at, peer], z_send.at[at, step], z_recv.at[at, peer], band, peer
+                ).wait_recv()
+                value += z_in[at, peer].astype(F32)
             planes[at, chip] = value.astype(BF)
             swaps.append([])
             for step, peer in enumerate(peers):
@@ -265,12 +295,12 @@
             final[at] = value
             final_copies[at].start()
             late_out[:, lo:hi] = value[:, : hi - lo]
-        ef_copy.wait_recv()
-        for copy in [e_copy] + final_copies + sum(moves, []) + sum(swaps, []):
+        for side, (_, out) in enumerate(sides):
+            ef_copies[side].wait_recv()
+            out[...] = e_final[side]
+        for copy in e_copies + final_copies + moves + sum(swaps, []):
             copy.wait_send()
 
-    recv_out[...] = e_final[:, :latents]
-    send_out[...] = e_final[:, latents:]
     for copy in rows + feats:
         copy.wait_send()
 
@@ -308,17 +338,18 @@
         send_index, edge_source, edge_receiver,
     )
     scratch = [
-        ((latents, grid), BF),
-        ((latents, grid), F32),
+        ((latents, inputs), BF),
+        ((latents, width), BF),
+        ((latents, slots), BF),
+        ((latents, slots), F32),
+        ((latents, slots), BF),
         ((2 * cap, width), BF),
         ((2 * cap, width), BF),
         ((2 * cap, wide), BF),
         ((2 * cap, wide), BF),
-        ((2 * cap, latents), BF),
-        ((2 * cap, latents), F32),
         ((2 * width, slots + mesh_count), BF),
-        ((steps, mesh_count, chunk), BF),
-        ((steps, slots, chunk), BF),
+        ((steps, mesh_count, chunk), jnp.float8_e4m3fn),
+        ((steps, slots, chunk), jnp.float8_e4m3fn),
         ((steps, 2 * width, chunk), F32),
         ((steps, 2 * width, chunk), BF),
         ((width, slots), F32),
@@ -327,18 +358,17 @@
         ((cuts, latents, LANES), BF),
         ((cuts, latents, LANES), BF),
         ((cuts, latents, LANES), BF),
-        ((cuts, chans - 1, width, LANES), BF),
+        ((cuts, chans, width, LANES), BF),
         ((cuts, chips, width, LANES), BF),
         ((cuts, width, LANES), F32),
-        ((width, 2 * latents), F32),
-        ((width, 2 * latents), BF),
-        ((width, 2 * latents), BF),
-        ((chips, width, 2 * latents), BF),
-        ((width, 2 * latents), F32),
+        ((2, width, latents), BF),
+        ((2, width, latents), BF),
+        ((2, chips, width, latents), BF),
+        ((2, width, latents), F32),
     ]
     sems = [
-        (2,), (2,), (2,), (2,), (cuts,), (cuts,), (cuts, chans - 1), (cuts, chans - 1),
-        (cuts, chips - 1), (cuts, chips - 1), (cuts,), (cuts,), (1,), (1,), (chips - 1,), (chips - 1,), (1,), (1,),
+        (2,), (2,), (2,), (2,), (cuts,), (cuts,), (cuts, chans - 1), (cuts, chans),
+        (cuts, chips - 1), (cuts, chips - 1), (cuts,), (cuts,), (2,), (2,), (2, chips - 1), (2, chips - 1), (2,), (2,),
     ]
     outs = pl.pallas_call(
         functools.partial(body, bands, chans, chunk),

time: 24.7 us -> 23.4 us (0.947)
  Pallas kernels: 23.9 us -> 22.6 us
    pallas_call x1, Pallas kernels: 23.1 us -> 21.8 us  [on_device(): pl.pallas_call(functools.partial(body, bands, chans, chunk), out_shape=(p...]
where the time goes in v2:
time: 23.4 us; the launch traced here: 23.3 us
  Pallas kernels  22.6 us (97%)
  between operations  0.64 us (3%)
    pallas_call x1, Pallas kernels, on_device(): pl.pallas_call(functools.partial(body, bands, chans, chunk), out_shape=(p...  21.8 us
    pallas_call x1, Pallas kernels, on_device(): pl.pallas_call(functools.partial(place, len(outs)), out_shape=tuple((jax....  0.83 us

profile of v2, /device:TPU:0, one launch (start us, length us, event | category | flops | bytes accessed | tf_op | source)
XLA Modules:
  0.0 23.3 jit_solution(17270834401062162177)
XLA Ops:
  0.6 21.8 %shard_map.120 = (bf16[96,256]{1,0:T(8,128)(2,1)S(1)}, f32[96,468]{1,0:T(8,128)S(1)}, f32[96,384]{1,0:T(8,128)S(1)}, f32[96,384]{1,0:T(8,128)S(1)}) custom-call(bf16[468,256]{1,0:T(8,128)(2,1)} %bitcast.8, bf16[468,384]{1,0:T(8,128)(2,1)} %embed_in.1, bf16[96,384]{1,0:T(8,128)(2,1)} %bitcast.9, bf16[96,384]{1,0:T(8,128)(2,1)} %bitcast.10, ...), custom_call_target="tpu_custom_call" | custom-call | tf_op jit(solution)/shard_map/pallas_call | solution.py:373
  22.4 0.8 %shard_map.121 = (bf16[96,256]{1,0:T(8,128)(2,1)}, f32[96,468]{1,0:T(8,128)}, f32[96,384]{1,0:T(8,128)}, f32[96,384]{1,0:T(8,128)}) custom-call(bf16[96,256]{1,0:T(8,128)(2,1)S(1)} %get-tuple-element.12.refs_0_, f32[96,468]{1,0:T(8,128)S(1)} %get-tuple-element.13.refs_1_, f32[96,384]{1,0:T(8,128)S(1)} %get-tuple-element.14.refs_2_, ...), custom_call_target="tpu_custom_call" | custom-call | tf_op jit(solution)/shard_map/pallas_call | solution.py:390

commit v3 on v2

--- a/solution.py
+++ b/solution.py
@@ -65,7 +65,7 @@
     left = lax.rem(band + bands - 1, bands)
     right = lax.rem(band + 1, bands)
     mate = band + 1 - 2 * core
-    peers = [2 * lax.rem(chip + step, chips) + core for step in range(1, chips)]
+    peers = [2 * (step + lax.min(lax.max(step + 1 - chip, 0), 1)) + core for step in range(chips - 1)]
     others = [lax.rem(chan + step, chans) for step in range(1, chans)]
     ordered = [step + lax.min(lax.max(step + 1 - chan, 0), 1) for step in range(chans - 1)]
 
@@ -97,33 +97,56 @@
         [send[0, 0:1, :], send[0, 1:2, :]], axis=1
     )
     pick_rows = jnp.transpose(jnp.where(picks, 1.0, 0.0)).astype(BF)
+    low, high = pl.ds(0, cap), pl.ds(cap, cap)
+
+    @pl.when(band == 0)
+    def _():
+        outer[low, :] = jnp.zeros((cap, width), BF)
+        feat_rows[low, :] = jnp.zeros((cap, feat_rows.shape[1]), BF)
+
+    @pl.when(band == bands - 1)
+    def _():
+        outer[high, :] = jnp.zeros((cap, width), BF)
+        feat_rows[high, :] = jnp.zeros((cap, feat_rows.shape[1]), BF)
+
     pulls["feat"].wait()
+    if inputs < feat_out.shape[1]:
+        feat_out[...] = jnp.zeros_like(feat_out)
+    listed = mm_nt(pick_rows, feat[...]).astype(BF)
+    feat_out[:, :inputs] = listed
     pulls["embed"].wait()
-    pre = mm_tn(embed[...], feat[...])
+    pre = mm(listed, embed[...])
+    listed = (pre * sigmoid(pre)).astype(BF)
+    pulls["wsend"].wait()
+    outgoing[...] = mm_nt(listed, wsend[...]).astype(BF)
+    pl.semaphore_wait(barrier, 3 + (chips - 1) + (chans - 1))
+    rows = [
+        remote(outgoing.at[low], outer.at[high], row_send.at[0], row_recv.at[0], left, chan),
+        remote(outgoing.at[high], outer.at[low], row_send.at[1], row_recv.at[1], right, chan),
+    ]
+    feats = [
+        remote(feat_out.at[low], feat_rows.at[high], feat_send.at[0], feat_recv.at[0], left, chan),
+        remote(feat_out.at[high], feat_rows.at[low], feat_send.at[1], feat_recv.at[1], right, chan),
+    ]
+    has_left, has_right = band > 0, band < bands - 1
+
+    @pl.when(has_left)
+    def _():
+        rows[0].start()
+        feats[0].start()
+
+    @pl.when(has_right)
+    def _():
+        rows[1].start()
+        feats[1].start()
+
+
+    embed_t[...] = jnp.transpose(embed[...])
+    pre = mm(embed_t[...], feat[...])
     gate = sigmoid(pre)
     silu = pre * gate
     latent[:, :grid] = silu.astype(BF)
-    pulls["wsend"].wait()
     own = mm(wsend[...], latent[:, :grid]).astype(BF)
-    outgoing[...] = mm_nt(pick_rows, own).astype(BF)
-    pl.semaphore_wait(barrier, 3 + (chips - 1) + (chans - 1))
-    low, high = pl.ds(0, cap), pl.ds(cap, cap)
-    rows = [
-        remote(outgoing.at[low], outer.at[high], row_send.at[0], row_recv.at[0], left, chan),
-        remote(outgoing.at[high], outer.at[low], row_send.at[1], row_recv.at[1], right, chan),
-    ]
-    for copy in rows:
-        copy.start()
-    if inputs < feat_out.shape[1]:
-        feat_out[...] = jnp.zeros_like(feat_out)
-    feat_out[:, :inputs] = mm_nt(pick_rows, feat[...]).astype(BF)
-    feats = [
-        remote(feat_out.at[low], feat_rows.at[high], feat_send.at[0], feat_recv.at[0], left, chan),
-        remote(feat_out.at[high], feat_rows.at[low], feat_send.at[1], feat_recv.at[1], right, chan),
-    ]
-    for copy in feats:
-        copy.start()
-
     slope[:, :grid] = gate + silu * (1.0 - gate)
     wsend_t[...] = mm_nt(eye(latents), wsend[...]).astype(BF)
     turn = eye(width)
@@ -143,9 +166,8 @@
         drawn[step] = mm(tables[:, slots:], hot_recv[step])
         hot_src[step] = one_hot(source, slots, step)
         drawn[step, :width, :] += mm(tables[:width, :grid], hot_src[step, :grid, :])
-    embed_t[...] = jnp.transpose(embed[...])
-    for copy in rows:
-        copy.wait_recv()
+    pl.when(has_right)(rows[0].wait_recv)
+    pl.when(has_left)(rows[1].wait_recv)
     tables[:width, grid:slots] = mm_nt(turn, outer[...]).astype(BF)
 
     for step in range(steps):
@@ -162,13 +184,14 @@
             acc[...] += mine
     total[...] = acc[...].astype(BF)
 
-    for copy in feats:
-        copy.wait_recv()
-    pre = mm_nt(embed_t[...], feat_rows[:, :inputs])
-    gate = sigmoid(pre)
-    silu = pre * gate
-    latent[:, grid:] = silu.astype(BF)
-    slope[:, grid:] = gate + silu * (1.0 - gate)
+    def finish_rows():
+        pl.when(has_right)(feats[0].wait_recv)
+        pl.when(has_left)(feats[1].wait_recv)
+        pre = mm_nt(embed_t[...], feat_rows[:, :inputs])
+        gate = sigmoid(pre)
+        silu = pre * gate
+        latent[:, grid:] = silu.astype(BF)
+        slope[:, grid:] = gate + silu * (1.0 - gate)
 
     def gradients():
         back[...] = (mm(wsend_t[...], total[...]) * slope[...]).astype(BF)
@@ -179,12 +202,14 @@
     def sender_part():
         return mm_nt(total[...], latent[...])
 
+    def receiver_sums(rows):
+        sums = mm_nt(pairs[0, rows, :], hot_recv[0])
+        for step in range(1, steps):
+            sums += mm_nt(pairs[step, rows, :], hot_recv[step])
+        return sums.astype(BF)
+
     def receiver_part():
-        sums = mm_nt(pairs[0], hot_recv[0])
-        for step in range(1, steps):
-            sums += mm_nt(pairs[step], hot_recv[step])
-        mesh_out[...] = sums[:width].astype(BF)
-        return mm(sums[width:].astype(BF), nodes[...])
+        return mm(receiver_sums(slice(width, 2 * width)), nodes[...])
 
     part_copies = [
         remote(part_out.at[at], part_in.at[at], part_send.at[at], part_recv.at[at], mate, chan)
@@ -204,6 +229,7 @@
 
     @pl.when(core == 0)
     def _():
+        finish_rows()
         gradients()
         for at, (lo, hi) in enumerate(cuts):
             if hi - lo < LANES:
@@ -218,14 +244,19 @@
             copies.append([])
             for at, peer in enumerate(peers):
                 copy = remote(
-                    e_planes.at[side, chip], e_planes.at[side, chip], ep_send.at[side, at], ep_recv.at[side, at],
+                    e_planes.at[side, chip], e_planes.at[side, chip], ep_send.at[side, at], ep_recv.at[side, chip],
                     peer, chan,
                 )
                 copy.start()
                 copies[side].append(copy)
+        mesh_out[...] = receiver_sums(slice(0, width))
         for side, (_, out) in enumerate(sides):
-            for copy in copies[side]:
-                copy.wait_recv()
+            for at, peer in enumerate(peers):
+                slot = lax.div(peer, 2)
+                remote(
+                    e_planes.at[side, slot], e_planes.at[side, slot], ep_send.at[side, at], ep_recv.at[side, slot],
+                    peer, chan,
+                ).wait_recv()
             value = e_planes[side, 0].astype(F32)
             for at in range(1, chips):
                 value += e_planes[side, at].astype(F32)
@@ -242,6 +273,7 @@
     def _():
         mine = pl.ds(pl.multiple_of(chan * width, width), width)
         first = pl.ds(pl.multiple_of(ordered[0] * width, width), width)
+        finish_rows()
         e_out[0] = sender_part().astype(BF)
         e_copies[0].start()
         gradients()
@@ -269,6 +301,7 @@
                 )
                 copy.start()
                 moves.append(copy)
+        mesh_out[...] = receiver_sums(slice(0, width))
         swaps = []
         for at, (lo, hi) in enumerate(cuts):
             value = z_out[at, mine, :].astype(F32)
@@ -281,28 +314,34 @@
             swaps.append([])
             for step, peer in enumerate(peers):
                 copy = remote(
-                    planes.at[at, chip], planes.at[at, chip], plane_send.at[at, step], plane_recv.at[at, step],
+                    planes.at[at, chip], planes.at[at, chip], plane_send.at[at, step], plane_recv.at[at, chip],
                     peer, chan,
                 )
                 copy.start()
                 swaps[at].append(copy)
         for at, (lo, hi) in enumerate(cuts):
-            for copy in swaps[at]:
-                copy.wait_recv()
+            for step, peer in enumerate(peers):
+                slot = lax.div(peer, 2)
+                remote(
+                    planes.at[at, slot], planes.at[at, slot], plane_send.at[at, step], plane_recv.at[at, slot],
+                    peer, chan,
+                ).wait_recv()
             value = planes[at, 0].astype(F32)
             for other in range(1, chips):
                 value += planes[at, other].astype(F32)
             final[at] = value
             final_copies[at].start()
-            late_out[:, lo:hi] = value[:, : hi - lo]
         for side, (_, out) in enumerate(sides):
             ef_copies[side].wait_recv()
             out[...] = e_final[side]
+        for at, (lo, hi) in enumerate(cuts):
+            late_out[:, lo:hi] = final[at, :, : hi - lo]
         for copy in e_copies + final_copies + moves + sum(swaps, []):
             copy.wait_send()
 
-    for copy in rows + feats:
-        copy.wait_send()
+    for has, at in ((has_left, 0), (has_right, 1)):
+        pl.when(has)(rows[at].wait_send)
+        pl.when(has)(feats[at].wait_send)
 
 
 def place(count, *refs):
@@ -328,7 +367,7 @@
     cap = send_index.shape[2]
     slots = grid + 2 * cap
     edges = edge_source.shape[0]
-    chunk = math.gcd(edges, 1024)
+    chunk = math.gcd(edges, 2048)
     steps = edges // chunk
     cuts = -(-inputs // LANES)
     wide = cuts * LANES
@@ -368,7 +407,7 @@
     ]
     sems = [
         (2,), (2,), (2,), (2,), (cuts,), (cuts,), (cuts, chans - 1), (cuts, chans),
-        (cuts, chips - 1), (cuts, chips - 1), (cuts,), (cuts,), (2,), (2,), (2, chips - 1), (2, chips - 1), (2,), (2,),
+        (cuts, chips - 1), (cuts, chips), (cuts,), (cuts,), (2,), (2,), (2, chips - 1), (2, chips), (2,), (2,),
     ]
     outs = pl.pallas_call(
         functools.partial(body, bands, chans, chunk),

time: 23.4 us -> 23 us (0.983)
  Pallas kernels: 22.6 us -> 22.2 us
    pallas_call x1, Pallas kernels: 21.8 us -> 21.3 us  [on_device(): pl.pallas_call(functools.partial(body, bands, chans, chunk), out_shape=(p...]
where the time goes in v3:
time: 23 us; the launch traced here: 22.8 us
  Pallas kernels  22.2 us (97%)
  between operations  0.64 us (3%)
    pallas_call x1, Pallas kernels, on_device(): pl.pallas_call(functools.partial(body, bands, chans, chunk), out_shape=(p...  21.3 us
    pallas_call x1, Pallas kernels, on_device(): pl.pallas_call(functools.partial(place, len(outs)), out_shape=tuple((jax....  0.83 us

profile of v3, /device:TPU:0, one launch (start us, length us, event | category | flops | bytes accessed | tf_op | source)
XLA Modules:
  0.0 22.8 jit_solution(16669377249067064354)
XLA Ops:
  0.6 21.3 %shard_map.120 = (bf16[96,256]{1,0:T(8,128)(2,1)S(1)}, f32[96,468]{1,0:T(8,128)S(1)}, f32[96,384]{1,0:T(8,128)S(1)}, f32[96,384]{1,0:T(8,128)S(1)}) custom-call(bf16[468,256]{1,0:T(8,128)(2,1)} %bitcast.8, bf16[468,384]{1,0:T(8,128)(2,1)} %embed_in.1, bf16[96,384]{1,0:T(8,128)(2,1)} %bitcast.9, bf16[96,384]{1,0:T(8,128)(2,1)} %bitcast.10, ...), custom_call_target="tpu_custom_call" | custom-call | tf_op jit(solution)/shard_map/pallas_call | solution.py:412
  22.0 0.8 %shard_map.121 = (bf16[96,256]{1,0:T(8,128)(2,1)}, f32[96,468]{1,0:T(8,128)}, f32[96,384]{1,0:T(8,128)}, f32[96,384]{1,0:T(8,128)}) custom-call(bf16[96,256]{1,0:T(8,128)(2,1)S(1)} %get-tuple-element.12.refs_0_, f32[96,468]{1,0:T(8,128)S(1)} %get-tuple-element.13.refs_1_, f32[96,384]{1,0:T(8,128)S(1)} %get-tuple-element.14.refs_2_, ...), custom_call_target="tpu_custom_call" | custom-call | tf_op jit(solution)/shard_map/pallas_call | solution.py:429

commit v4 on v3

--- a/solution.py
+++ b/solution.py
@@ -66,7 +66,6 @@
     right = lax.rem(band + 1, bands)
     mate = band + 1 - 2 * core
     peers = [2 * (step + lax.min(lax.max(step + 1 - chip, 0), 1)) + core for step in range(chips - 1)]
-    others = [lax.rem(chan + step, chans) for step in range(1, chans)]
     ordered = [step + lax.min(lax.max(step + 1 - chan, 0), 1) for step in range(chans - 1)]
 
     pulls = {}
@@ -83,8 +82,12 @@
     barrier = pltpu.get_barrier_semaphore()
     for peer in [left, right, mate] + peers:
         pl.semaphore_signal(barrier, inc=1, device_id=(peer, chan), device_id_type=MESH)
-    for peer in others:
-        pl.semaphore_signal(barrier, inc=1, device_id=(band, peer), device_id_type=MESH)
+
+    @pl.when(core == 1)
+    def _():
+        for peer in ordered:
+            pl.semaphore_signal(barrier, inc=1, device_id=(band, peer), device_id_type=MESH)
+
 
     def remote(src, dst, send_sem, recv_sem, to_band, to_chan):
         return pltpu.make_async_remote_copy(
@@ -119,7 +122,7 @@
     listed = (pre * sigmoid(pre)).astype(BF)
     pulls["wsend"].wait()
     outgoing[...] = mm_nt(listed, wsend[...]).astype(BF)
-    pl.semaphore_wait(barrier, 3 + (chips - 1) + (chans - 1))
+    pl.semaphore_wait(barrier, 3 + (chips - 1) + core * (chans - 1))
     rows = [
         remote(outgoing.at[low], outer.at[high], row_send.at[0], row_recv.at[0], left, chan),
         remote(outgoing.at[high], outer.at[low], row_send.at[1], row_recv.at[1], right, chan),

time: 23 us -> 22.1 us (0.961)
  Pallas kernels: 22.2 us -> 21.3 us
    pallas_call x1, Pallas kernels: 21.3 us -> 20.5 us  [on_device(): pl.pallas_call(functools.partial(body, bands, chans, chunk), out_shape=(p...]
where the time goes in v4:
time: 22.1 us; the launch traced here: 22 us
  Pallas kernels  21.3 us (96%)
  between operations  0.64 us (3%)
    pallas_call x1, Pallas kernels, on_device(): pl.pallas_call(functools.partial(body, bands, chans, chunk), out_shape=(p...  20.5 us
    pallas_call x1, Pallas kernels, on_device(): pl.pallas_call(functools.partial(place, len(outs)), out_shape=tuple((jax....  0.83 us

profile of v4, /device:TPU:0, one launch (start us, length us, event | category | flops | bytes accessed | tf_op | source)
XLA Modules:
  0.0 22.0 jit_solution(409593789070864651)
XLA Ops:
  0.6 20.5 %shard_map.120 = (bf16[96,256]{1,0:T(8,128)(2,1)S(1)}, f32[96,468]{1,0:T(8,128)S(1)}, f32[96,384]{1,0:T(8,128)S(1)}, f32[96,384]{1,0:T(8,128)S(1)}) custom-call(bf16[468,256]{1,0:T(8,128)(2,1)} %bitcast.8, bf16[468,384]{1,0:T(8,128)(2,1)} %embed_in.1, bf16[96,384]{1,0:T(8,128)(2,1)} %bitcast.9, bf16[96,384]{1,0:T(8,128)(2,1)} %bitcast.10, ...), custom_call_target="tpu_custom_call" | custom-call | tf_op jit(solution)/shard_map/pallas_call | solution.py:415
  21.1 0.8 %shard_map.121 = (bf16[96,256]{1,0:T(8,128)(2,1)}, f32[96,468]{1,0:T(8,128)}, f32[96,384]{1,0:T(8,128)}, f32[96,384]{1,0:T(8,128)}) custom-call(bf16[96,256]{1,0:T(8,128)(2,1)S(1)} %get-tuple-element.12.refs_0_, f32[96,468]{1,0:T(8,128)S(1)} %get-tuple-element.13.refs_1_, f32[96,384]{1,0:T(8,128)S(1)} %get-tuple-element.14.refs_2_, ...), custom_call_target="tpu_custom_call" | custom-call | tf_op jit(solution)/shard_map/pallas_call | solution.py:432
